TPU v7x, 32 devices: a whole 2x2x4 slice. The times are simulated.
32 devices in a mesh: member: 4 (over y, x), dom: 8 (over z, core).
Axes of the slice: x: 2, y: 2, z: 4, core: 2. Of those that a mesh axis runs over, the one named last changes fastest.
Arguments:
- acoustic_perturbation: float32 [4, 32, 8192], P('member', None, 'dom'), may hold values from -8 to 8
- prior_acoustic_state: float32 [4, 32, 8192], P('member', None, 'dom'), may hold values from -8 to 8
- thermal_anomaly: float32 [4, 32, 8192], P('member', None, 'dom'), may hold values from -8 to 8
- model_parameters: float32 [4, 4], P('member'), may hold values from 0.5 to 1.5
- crossing_velocity: float32 [32, 24576], P(None, 'dom'), may hold values from -3 to 3
- face_extent: float32 [24576], P('dom'), may hold values from 0.1 to 0.4
- face_metric_factor: float32 [24576], P('dom'), may hold values from 0.01 to 0.06
- reciprocal_polygon_surface: float32 [8192], P('dom'), may hold values from 0.5 to 2
- owned_totals: int32 [8], P('dom'), may hold values from 768 to 1024, as said below
- export_lists: int32 [8, 6, 128], P('dom'), may hold values from 0 to 1024, as said below
- face_neighbour_pair: int32 [2, 24576], P(None, 'dom'), may hold values from 0 to 1792, as said below
- polygon_side_lookup: int32 [6, 8192], P(None, 'dom'), may hold values from 0 to 3072, as said below
Outputs:
- pressure_out: float32 [4, 32, 8192], P('member', None, 'dom')
- temperature_out: float32 [4, 32, 8192], P('member', None, 'dom')
- ensemble_mean: float32 [32, 8192], P(None, 'dom')
Inputs may be any that keep to these rules, and one draw needn't show every extreme that they name: The first owned_totals[p] cell slots of partition p are its cells, the rest unused; some partition has 1024. Row export_lists[p, b] lists owned cells of partition p sent to partition (p + offsets[b]) mod 8; filled entries first, then 1024 in the empty slots; at least 64 filled entries a row; in every draw some partition receives 128 filled entries in all 6 of its rows. `face_neighbour_pair`: edge 3 i + j of partition p starts at owned cell i and ends at another owned cell or at halo column 1024 + b * 128 + k whose slot k is filled in the sender's row b; edges of unused cells have both ends at 1792. `polygon_side_lookup`: the local edges with an end at each owned cell, 3072 in empty slots; unused cells have only empty slots.
All inputs are finite; a program needn't handle non-finite values.
Results may differ from a plain program's by a relative error of at most 0.0001.
Values sent between devices are 32-bit elements; how exact they have to be, the bound alone decides.
A program may use at most 64 MiB of HBM per device.

v0:
```python
import math
import jax
import jax.numpy as jnp
from jax import lax
from jax.sharding import PartitionSpec as P

STEPS = 2
NS = 3
time_step = 0.25


def passed_along(block, axis, distance):
    devices = range(lax.axis_size(axis))
    route = [((i - distance) % len(devices), i) for i in devices]
    return lax.ppermute(block, axis, route)


def neighbour_offsets(count):
    return [(block_number // 2 + 1) * (1 - 2 * (block_number % 2)) for block_number in range(count)]


def exact_dot(left_side, right_side):
    return jnp.dot(
        left_side, right_side, precision=lax.Precision.HIGHEST, preferred_element_type=jnp.float32
    )


def edge_block_size(edge_count):
    return math.gcd(edge_count, 384)


def gather_ends(extended, finish):
    edge_count = finish.shape[0]
    block_size = edge_block_size(edge_count)
    column_count = extended.shape[1]
    index_blocks = finish.reshape(edge_count // block_size, block_size)

    def one_block(indices):
        selector = (
            lax.broadcasted_iota(jnp.int32, (column_count, block_size), 0) == indices[None, :]
        ).astype(jnp.float32)
        return exact_dot(extended, selector)

    blocks = lax.map(one_block, index_blocks)
    return jnp.transpose(blocks, (1, 0, 2)).reshape(extended.shape[0], edge_count)


def divergence(fluxes, finish, cell_count):
    levels = fluxes.shape[0]
    edge_count = fluxes.shape[1]
    block_size = edge_block_size(edge_count)
    block_count = edge_count // block_size
    index_blocks = finish.reshape(block_count, block_size)
    flux_blocks = jnp.transpose(fluxes.reshape(levels, block_count, block_size), (1, 0, 2))

    def add_block(total, items):
        indices, flux_piece = items
        selector = (
            indices[:, None] == lax.broadcasted_iota(jnp.int32, (block_size, cell_count), 1)
        ).astype(jnp.float32)
        return (total + exact_dot(flux_piece, selector), None)

    incoming, unused = lax.scan(
        add_block, jnp.zeros((levels, cell_count), jnp.float32), (index_blocks, flux_blocks)
    )
    outgoing = jnp.sum(fluxes.reshape(levels, cell_count, 3), axis=2)
    return outgoing - incoming


def outgoing_rows(fields, export_lists):
    listed = export_lists[0].reshape(-1)
    selector = (
        lax.broadcasted_iota(jnp.int32, (fields.shape[1], listed.shape[0]), 0) == listed[None, :]
    ).astype(jnp.float32)
    chosen = exact_dot(fields, selector)
    zero_column = jnp.zeros((fields.shape[0], 1), jnp.float32)
    return (
        chosen.reshape(fields.shape[0], export_lists.shape[1], export_lists.shape[2]),
        zero_column,
    )


def extend(fields, export_lists):
    outgoing, zero_column = outgoing_rows(fields, export_lists)
    dom_count = lax.axis_size("dom")
    pieces = []
    for block_number, offset in enumerate(neighbour_offsets(export_lists.shape[1])):
        pieces.append(passed_along(outgoing[:, block_number], "dom", offset % dom_count))
    return jnp.concatenate([fields] + pieces + [zero_column], axis=1)


def starts_of(fields):
    levels = fields.shape[0]
    cell_count = fields.shape[1]
    return jnp.broadcast_to(fields[:, :, None], (levels, cell_count, 3)).reshape(
        levels, 3 * cell_count
    )


def per_device(
    acoustic_perturbation,
    prior_acoustic_state,
    thermal_anomaly,
    model_parameters,
    crossing_velocity,
    face_extent,
    face_metric_factor,
    reciprocal_polygon_surface,
    owned_totals,
    export_lists,
    face_neighbour_pair,
    polygon_side_lookup,
):
    levels = acoustic_perturbation.shape[1]
    cell_count = acoustic_perturbation.shape[2]
    current = acoustic_perturbation[0]
    previous = prior_acoustic_state[0]
    scalar_quantity = thermal_anomaly[0]
    speed = model_parameters[0, 0]
    kappa = 0.5 * model_parameters[0, 1]
    mixing = 0.6 * model_parameters[0, 2]
    couple = model_parameters[0, 3]
    owned = (jnp.arange(cell_count, dtype=jnp.int32) < owned_totals[0])[None, :]
    cell_area = jnp.where(owned[0], 1.0 / reciprocal_polygon_surface, 0.0)
    finish = face_neighbour_pair[1]
    inverse = reciprocal_polygon_surface[None, :]
    for outer_step in range(STEPS):
        extended = extend(jnp.concatenate([scalar_quantity, current], axis=0), export_lists)
        theta_ext = extended[:levels]
        press_ext = extended[levels:]
        left = starts_of(scalar_quantity)
        right = gather_ends(theta_ext, finish)
        fluxes = face_extent[None, :] * (
            0.5 * crossing_velocity * (left + right)
            - (0.5 * jnp.abs(crossing_velocity) + kappa) * (right - left)
        )
        differences = scalar_quantity[1:] - scalar_quantity[:-1]
        zero_row = jnp.zeros((1, cell_count), jnp.float32)
        vertical = mixing * (
            jnp.concatenate([differences, zero_row], 0)
            - jnp.concatenate([zero_row, differences], 0)
        )
        advanced = jnp.where(
            owned,
            scalar_quantity
            + time_step * (-inverse * divergence(fluxes, finish, cell_count) + vertical),
            scalar_quantity,
        )
        forcing = couple * (advanced - scalar_quantity) / NS
        for substep in range(NS):
            if substep > 0:
                press_ext = extend(current, export_lists)
            gradient = face_metric_factor[None, :] * (
                gather_ends(press_ext, finish) - starts_of(current)
            )
            stepped = jnp.where(
                owned,
                2.0 * current
                - previous
                + speed * inverse * divergence(gradient, finish, cell_count)
                + forcing,
                current,
            )
            previous, current = (current, stepped)
        weighted, area_total = lax.psum(
            (jnp.sum(current * cell_area[None, :], axis=1), jnp.sum(cell_area)), "dom"
        )
        level_mean = (weighted / area_total)[:, None]
        current = jnp.where(owned, current - level_mean, current)
        previous = jnp.where(owned, previous - level_mean, previous)
        scalar_quantity = advanced
    ensemble = lax.psum(current, "member") / lax.axis_size("member")
    return (current[None], scalar_quantity[None], ensemble)


def solution(mesh):
    in_specs = (
        P("member", None, "dom"),
        P("member", None, "dom"),
        P("member", None, "dom"),
        P("member", None),
        P(None, "dom"),
        P("dom"),
        P("dom"),
        P("dom"),
        P("dom"),
        P("dom", None, None),
        P(None, "dom"),
        P(None, "dom"),
    )
    out_specs = (P("member", None, "dom"), P("member", None, "dom"), P(None, "dom"))
    return jax.shard_map(
        per_device, mesh=mesh, in_specs=in_specs, out_specs=out_specs, check_vma=False
    )
```

profile of v0, /device:TPU:0, one launch (start us, length us, event | category | flops | bytes accessed | tf_op | source)
XLA Modules:
  0.0 611.0 jit_solution(15316306464230908391)
XLA Ops:
  14.2 4.0 collective-permute-start.1
  30.6 3.8 reshape.204
  58.2 9.1 %while.168 = (s32[]{:T(128)}, f32[8,32,384]{2,1,0:T(8,128)S(1)}, s32[8,384]{1,0:T(8,128)S(1)}, f32[32,1793]{1,0:T(8,128)S(1)}, s32[]{:T(128)}) while((s32[]{:T(128)}, f32[8,32,384]{2,1,0:T(8,128)S(1)}, s32[8,384]{1,0:T(8,128)S(1)}, f32[32,1793]{1,0:T(8,128)S(1)}, s32[]{:T(128)}) %tuple.345), condition=%wide.region_1.2_spmd, body=%wide.region_0.1_spmd.sunk | while | flops 265077120 | bytes 300101 | solution.py:44
  72.6 23.0 %while.176 = (s32[]{:T(128)}, f32[32,1024]{1,0:T(8,128)}, f32[8,32,384]{2,1,0:T(8,128)S(1)}, s32[8,384]{1,0:T(8,128)S(1)}, s32[]{:T(128)}, /*index=5*/s32[]{:T(128)}) while((s32[]{:T(128)}, f32[32,1024]{1,0:T(8,128)}, f32[8,32,384]{2,1,0:T(8,128)S(1)}, s32[8,384]{1,0:T(8,128)S(1)}, s32[]{:T(128)}, /*index=5*/s32[]{:T(128)}) %tuple.395), condition=%wide.region_4.5_spmd.clone, body=%wide.region_3.4_spmd.clone.sunk | while | flops 151453696 | bytes 315991 | solution.py:63
  99.7 16.6 %while.169 = (s32[]{:T(128)}, f32[8,32,384]{2,1,0:T(8,128)S(1)}, s32[8,384]{1,0:T(8,128)S(1)}, f32[32,1793]{1,0:T(8,128)}, s32[]{:T(128)}) while((s32[]{:T(128)}, f32[8,32,384]{2,1,0:T(8,128)S(1)}, s32[8,384]{1,0:T(8,128)S(1)}, f32[32,1793]{1,0:T(8,128)}, s32[]{:T(128)}) %tuple.396), condition=%wide.region_6.7_spmd, body=%wide.region_5.6_spmd.sunk | while | flops 265077120 | bytes 283845 | solution.py:44
  120.1 25.9 %while.177 = (s32[]{:T(128)}, f32[32,1024]{1,0:T(8,128)}, f32[8,32,384]{2,0,1:T(8,128)}, s32[8,384]{1,0:T(8,128)S(1)}, s32[]{:T(128)}, /*index=5*/s32[]{:T(128)}) while((s32[]{:T(128)}, f32[32,1024]{1,0:T(8,128)}, f32[8,32,384]{2,0,1:T(8,128)}, s32[8,384]{1,0:T(8,128)S(1)}, s32[]{:T(128)}, /*index=5*/s32[]{:T(128)}) %tuple.410), condition=%wide.region_9.10_spmd.clone, body=%wide.region_8.9_spmd.clone.sunk | while | flops 151453696 | bytes 414295 | solution.py:63
  149.6 3.7 reshape.207
  153.3 7.6 %multiply_reduce_fusion.5 = f32[32,1024]{0,1:T(8,128)} fusion(f32[32,1024,3]{0,2,1:T(4,128)} %reshape.203, f32[32,1024]{0,1:T(8,128)S(1)} %bitcast.284, f32[1024,3]{1,0:T(8,128)S(1)} %mul.239), kind=kLoop, calls=%fused_computation.122 | loop fusion | flops 262144 | bytes 667648 | tf_op jit(solution)/shard_map/reduce_sum | solution.py:66
  160.9 3.7 reduce_sum.104
  169.5 3.7 collective-permute-start.7
  174.9 3.8 collective-permute-start.9
  180.4 3.8 reshape.211
  185.9 3.8 reshape.218
  199.3 16.6 %while.170 = (s32[]{:T(128)}, f32[8,32,384]{2,1,0:T(8,128)S(1)}, s32[8,384]{1,0:T(8,128)S(1)}, f32[32,1793]{1,0:T(8,128)}, s32[]{:T(128)}) while((s32[]{:T(128)}, f32[8,32,384]{2,1,0:T(8,128)S(1)}, s32[8,384]{1,0:T(8,128)S(1)}, f32[32,1793]{1,0:T(8,128)}, s32[]{:T(128)}) %tuple.398), condition=%wide.region_11.12_spmd, body=%wide.region_10.11_spmd.sunk | while | flops 265077120 | bytes 283845 | solution.py:44
  222.9 6.2 %while.178 = (s32[]{:T(128)}, f32[32,1024]{1,0:T(8,128)S(1)}, f32[8,32,384]{2,1,0:T(8,128)S(1)}, s32[8,384]{1,0:T(8,128)S(1)}, s32[]{:T(128)}, /*index=5*/s32[]{:T(128)}) while((s32[]{:T(128)}, f32[32,1024]{1,0:T(8,128)S(1)}, f32[8,32,384]{2,1,0:T(8,128)S(1)}, s32[8,384]{1,0:T(8,128)S(1)}, s32[]{:T(128)}, ...), condition=%wide.region_14.15_spmd.clone, body=%wide.region_13.14_spmd.clone.sunk | while | flops 151453696 | bytes 316503 | solution.py:63
  230.2 3.7 reshape.210
  233.9 6.9 %multiply_reduce_fusion.4 = f32[32,1024]{0,1:T(8,128)S(1)} fusion(f32[32,1024,3]{0,2,1:T(4,128)} %reshape.210, f32[32,1024]{0,1:T(8,128)S(1)} %get-tuple-element.831, f32[1024,3]{1,0:T(8,128)S(1)} %mul.239), kind=kLoop, calls=%fused_computation.121 | loop fusion | flops 262144 | bytes 667648 | tf_op jit(solution)/shard_map/reduce_sum | solution.py:66
  242.7 3.6 collective-permute-start.13
  246.2 3.8 collective-permute-start.15
  251.8 3.8 reshape.214
  259.9 9.0 %while.171 = (s32[]{:T(128)}, f32[8,32,384]{2,1,0:T(8,128)S(1)}, s32[8,384]{1,0:T(8,128)S(1)}, f32[32,1793]{1,0:T(8,128)S(1)}, s32[]{:T(128)}) while((s32[]{:T(128)}, f32[8,32,384]{2,1,0:T(8,128)S(1)}, s32[8,384]{1,0:T(8,128)S(1)}, f32[32,1793]{1,0:T(8,128)S(1)}, s32[]{:T(128)}) %tuple.400), condition=%wide.region_16.17_spmd, body=%wide.region_15.16_spmd.sunk | while | flops 265077120 | bytes 300101 | solution.py:44
  276.0 6.2 %while.179 = (s32[]{:T(128)}, f32[32,1024]{1,0:T(8,128)S(1)}, f32[8,32,384]{2,1,0:T(8,128)S(1)}, s32[8,384]{1,0:T(8,128)S(1)}, s32[]{:T(128)}, /*index=5*/s32[]{:T(128)}) while((s32[]{:T(128)}, f32[32,1024]{1,0:T(8,128)S(1)}, f32[8,32,384]{2,1,0:T(8,128)S(1)}, s32[8,384]{1,0:T(8,128)S(1)}, s32[]{:T(128)}, ...), condition=%wide.region_19.20_spmd.clone, body=%wide.region_18.19_spmd.clone.sunk | while | flops 151453696 | bytes 316503 | solution.py:63
  283.3 3.7 reshape.213
  286.9 6.9 %multiply_reduce_fusion.3 = f32[32,1024]{0,1:T(8,128)S(1)} fusion(f32[32,1024,3]{0,2,1:T(4,128)} %reshape.213, f32[32,1024]{0,1:T(8,128)S(1)} %add_select_fusion.5, f32[1024,3]{1,0:T(8,128)S(1)} %mul.239), kind=kLoop, calls=%fused_computation.120 | loop fusion | flops 262144 | bytes 667648 | tf_op jit(solution)/shard_map/reduce_sum | solution.py:66
  294.8 14.8 %all-reduce.4 = (f32[32]{0:T(128)S(1)}, f32[]{:T(128)}) all-reduce(f32[32]{0:T(128)S(1)} %get-tuple-element.829, f32[]{:T(128)} %get-tuple-element.876), channel_id=1, replica_groups=mesh['member'=4,'dom'=8] {'dom'}, use_global_device_ids=true, to_apply=%region_21.22 | all-reduce | flops 33 | bytes 264 | tf_op jit(solution)/shard_map/psum | solution.py:165
  319.2 3.8 collective-permute-start.21
  324.7 3.8 reshape.217
  341.5 17.0 %while.173 = (s32[]{:T(128)}, f32[8,32,384]{2,1,0:T(8,128)S(1)}, s32[8,384]{1,0:T(8,128)S(1)}, f32[32,1793]{1,0:T(8,128)}, s32[]{:T(128)}) while((s32[]{:T(128)}, f32[8,32,384]{2,1,0:T(8,128)S(1)}, s32[8,384]{1,0:T(8,128)S(1)}, f32[32,1793]{1,0:T(8,128)}, s32[]{:T(128)}) %tuple.402), condition=%wide.region_30.31_spmd, body=%wide.region_29.30_spmd.sunk | while | flops 265077120 | bytes 283845 | solution.py:44
  361.3 3.7 reshape.220
  365.8 14.6 %while.181 = (s32[]{:T(128)}, f32[32,1024]{1,0:T(8,128)S(1)}, f32[8,32,384]{2,0,1:T(8,128)}, s32[8,384]{1,0:T(8,128)S(1)}, s32[]{:T(128)}, /*index=5*/s32[]{:T(128)}) while((s32[]{:T(128)}, f32[32,1024]{1,0:T(8,128)S(1)}, f32[8,32,384]{2,0,1:T(8,128)}, s32[8,384]{1,0:T(8,128)S(1)}, s32[]{:T(128)}, /*index=5*/s32[]{:T(128)}) %tuple.414), condition=%wide.region_33.34_spmd.clone, body=%wide.region_32.33_spmd.clone.sunk | while | flops 151453696 | bytes 414295 | solution.py:63
  382.9 9.1 %while.172 = (s32[]{:T(128)}, f32[8,32,384]{2,1,0:T(8,128)S(1)}, s32[8,384]{1,0:T(8,128)S(1)}, f32[32,1793]{1,0:T(8,128)S(1)}, s32[]{:T(128)}) while((s32[]{:T(128)}, f32[8,32,384]{2,1,0:T(8,128)S(1)}, s32[8,384]{1,0:T(8,128)S(1)}, f32[32,1793]{1,0:T(8,128)S(1)}, s32[]{:T(128)}) %tuple.404), condition=%wide.region_25.26_spmd, body=%wide.region_24.25_spmd.sunk | while | flops 265077120 | bytes 300101 | solution.py:44
  399.1 6.2 %while.180 = (s32[]{:T(128)}, f32[32,1024]{1,0:T(8,128)S(1)}, f32[8,32,384]{2,1,0:T(8,128)S(1)}, s32[8,384]{1,0:T(8,128)S(1)}, s32[]{:T(128)}, /*index=5*/s32[]{:T(128)}) while((s32[]{:T(128)}, f32[32,1024]{1,0:T(8,128)S(1)}, f32[8,32,384]{2,1,0:T(8,128)S(1)}, s32[8,384]{1,0:T(8,128)S(1)}, s32[]{:T(128)}, ...), condition=%wide.region_28.29_spmd.clone, body=%wide.region_27.28_spmd.clone.sunk | while | flops 151453696 | bytes 316503 | solution.py:63
  406.4 3.7 reshape.216
  410.0 7.6 %multiply_reduce_fusion.2 = f32[32,1024]{0,1:T(8,128)} fusion(f32[32,1024,3]{0,2,1:T(4,128)} %reshape.216, f32[32,1024]{0,1:T(8,128)S(1)} %subtract_select_fusion.2, f32[1024,3]{1,0:T(8,128)S(1)} %mul.239), kind=kLoop, calls=%fused_computation.119 | loop fusion | flops 262144 | bytes 667648 | tf_op jit(solution)/shard_map/reduce_sum | solution.py:66
  417.7 3.8 reduce_sum.110
  421.5 3.6 fusion.89
  430.7 3.8 collective-permute-start.27
  443.5 9.1 %while.174 = (s32[]{:T(128)}, f32[8,32,384]{2,1,0:T(8,128)S(1)}, s32[8,384]{1,0:T(8,128)S(1)}, f32[32,1793]{1,0:T(8,128)S(1)}, s32[]{:T(128)}) while((s32[]{:T(128)}, f32[8,32,384]{2,1,0:T(8,128)S(1)}, s32[8,384]{1,0:T(8,128)S(1)}, f32[32,1793]{1,0:T(8,128)S(1)}, s32[]{:T(128)}) %tuple.406), condition=%wide.region_35.36_spmd, body=%wide.region_34.35_spmd.sunk | while | flops 265077120 | bytes 300101 | solution.py:44
  458.0 6.2 %while.182 = (s32[]{:T(128)}, f32[32,1024]{1,0:T(8,128)S(1)}, f32[8,32,384]{2,1,0:T(8,128)S(1)}, s32[8,384]{1,0:T(8,128)S(1)}, s32[]{:T(128)}, /*index=5*/s32[]{:T(128)}) while((s32[]{:T(128)}, f32[32,1024]{1,0:T(8,128)S(1)}, f32[8,32,384]{2,1,0:T(8,128)S(1)}, s32[8,384]{1,0:T(8,128)S(1)}, s32[]{:T(128)}, ...), condition=%wide.region_38.39_spmd.clone, body=%wide.region_37.38_spmd.clone.sunk | while | flops 151453696 | bytes 316503 | solution.py:63
  466.9 7.0 %multiply_reduce_fusion.1 = f32[32,1024]{0,1:T(8,128)S(1)} fusion(f32[32,1024,3]{0,2,1:T(4,128)} %reshape.223, f32[32,1024]{0,1:T(8,128)S(1)} %get-tuple-element.824, f32[1024,3]{1,0:T(8,128)S(1)} %mul.239), kind=kLoop, calls=%fused_computation.118 | loop fusion | flops 262144 | bytes 667648 | tf_op jit(solution)/shard_map/reduce_sum | solution.py:66
  475.8 3.6 collective-permute-start.31
  479.3 3.8 collective-permute-start.33
  484.9 3.8 reshape.227
  493.0 9.0 %while.175 = (s32[]{:T(128)}, f32[8,32,384]{2,1,0:T(8,128)S(1)}, s32[8,384]{1,0:T(8,128)S(1)}, f32[32,1793]{1,0:T(8,128)S(1)}, s32[]{:T(128)}) while((s32[]{:T(128)}, f32[8,32,384]{2,1,0:T(8,128)S(1)}, s32[8,384]{1,0:T(8,128)S(1)}, f32[32,1793]{1,0:T(8,128)S(1)}, s32[]{:T(128)}) %tuple.408), condition=%wide.region_40.41_spmd, body=%wide.region_39.40_spmd.sunk | while | flops 265077120 | bytes 300101 | solution.py:44
  507.4 23.0 %while.183 = (s32[]{:T(128)}, f32[32,1024]{1,0:T(8,128)}, f32[8,32,384]{2,1,0:T(8,128)S(1)}, s32[8,384]{1,0:T(8,128)S(1)}, s32[]{:T(128)}, /*index=5*/s32[]{:T(128)}) while((s32[]{:T(128)}, f32[32,1024]{1,0:T(8,128)}, f32[8,32,384]{2,1,0:T(8,128)S(1)}, s32[8,384]{1,0:T(8,128)S(1)}, s32[]{:T(128)}, /*index=5*/s32[]{:T(128)}) %tuple.409), condition=%wide.region_43.44_spmd.clone, body=%wide.region_42.43_spmd.clone.sunk | while | flops 151453696 | bytes 315991 | solution.py:63
  534.0 6.9 %multiply_reduce_fusion = f32[32,1024]{0,1:T(8,128)S(1)} fusion(f32[32,1024,3]{0,2,1:T(4,128)} %reshape.226, f32[32,1024]{0,1:T(8,128)S(1)} %add_select_fusion.3, f32[1024,3]{1,0:T(8,128)S(1)} %mul.239), kind=kLoop, calls=%fused_computation.117 | loop fusion | flops 262144 | bytes 667648 | tf_op jit(solution)/shard_map/reduce_sum | solution.py:66
  541.9 14.2 %psum.33 = f32[32]{0:T(128)S(1)} all-reduce(f32[32]{0:T(128)S(1)} %get-tuple-element.822), channel_id=1, replica_groups=mesh['member'=4,'dom'=8] {'dom'}, use_global_device_ids=true, to_apply=%region_45.46 | all-reduce | flops 32 | bytes 256 | tf_op jit(solution)/shard_map/psum | solution.py:165
  558.8 43.2 %all-reduce.7.cloned.1.call-done = f32[32,1024]{0,1:T(8,128)} async-done(((f32[32,1024]{0,1:T(8,128)}), f32[32,1024]{0,1:T(8,128)}) %all-reduce.7.cloned.1.call-update) | async-done | bytes 131088 | tf_op jit(solution)/shard_map/psum | solution.py:172
  (590 shorter events, 389.2 us)
Async XLA Ops:
  7.2 594.8 %all-reduce.7.cloned.1.call-start = ((), (), s32[]{:S(2)}) async-start(), calls=%async_computation | async-start | bytes 1048576 | tf_op jit(solution)/shard_map/psum | solution.py:172
  10.1 12.9 %copy-start.35 = (s32[6,128]{1,0:T(8,128)}, s32[6,128]{1,0:T(8,128)S(1)}, u32[]{:S(2)}) copy-start(s32[6,128]{1,0:T(8,128)S(1)} %reduce.17) | copy-start | bytes 9220
  12.9 11.1 %copy-start.31 = (s32[2,3072]{1,0:T(2,128)S(1)}, s32[2,3072]{1,0:T(2,128)}, u32[]{:S(2)}) copy-start(s32[2,3072]{1,0:T(2,128)} %param.54) | copy-start | bytes 73732
  13.0 11.1 %copy-start.30 = (f32[1,4]{1,0:T(1,128)S(1)}, f32[1,4]{1,0:T(1,128)}, u32[]{:S(2)}) copy-start(f32[1,4]{1,0:T(1,128)} %param.47) | copy-start | bytes 52
  13.0 12.4 %copy-start.40 = (f32[1024]{0:T(1024)S(1)}, f32[1024]{0:T(1024)}, u32[]{:S(2)}) copy-start(f32[1024]{0:T(1024)} %param.51) | copy-start | bytes 12292
  13.0 14.9 %copy-start.25 = (f32[3072]{0:T(1024)S(1)}, f32[3072]{0:T(1024)}, u32[]{:S(2)}) copy-start(f32[3072]{0:T(1024)} %param.50) | copy-start | bytes 36868
  13.7 28.6 %collective-permute-start = (f32[64,128]{0,1:T(8,128)}, f32[64,128]{0,1:T(8,128)}, u32[]{:S(2)}, u32[]{:S(2)}) collective-permute-start(f32[64,128]{0,1:T(8,128)} %get-tuple-element.849), channel_id=1, source_target_pairs={{7,0},{0,1},{1,2},{2,3},{3,4},{4,5},{5,6},{6,7},{15,8},{8,9},{9,10... | collective-permute-start | bytes 98312 | tf_op jit(solution)/shard_map/ppermute | solution.py:15
  14.2 32.7 %collective-permute-start.1 = (f32[64,128]{0,1:T(8,128)}, f32[64,128]{0,1:T(8,128)}, u32[]{:S(2)}, u32[]{:S(2)}) collective-permute-start(f32[64,128]{0,1:T(8,128)} %get-tuple-element.848), channel_id=1, source_target_pairs={{1,0},{2,1},{3,2},{4,3},{5,4},{6,5},{7,6},{0,7},{9,8},{10,9},{11,1... | collective-permute-start | bytes 98312 | tf_op jit(solution)/shard_map/ppermute | solution.py:15
  18.2 30.1 %collective-permute-start.2 = (f32[64,128]{0,1:T(8,128)S(1)}, f32[64,128]{0,1:T(8,128)}, u32[]{:S(2)}, u32[]{:S(2)}) collective-permute-start(f32[64,128]{0,1:T(8,128)S(1)} %get-tuple-element.847), channel_id=1, source_target_pairs={{6,0},{7,1},{0,2},{1,3},{2,4},{3,5},{4,6},{5,7},{14,8},{15,9},{8,1... | collective-permute-start | bytes 98312 | tf_op jit(solution)/shard_map/ppermute | solution.py:15
  18.5 31.3 %collective-permute-start.3 = (f32[64,128]{0,1:T(8,128)S(1)}, f32[64,128]{0,1:T(8,128)}, u32[]{:S(2)}, u32[]{:S(2)}) collective-permute-start(f32[64,128]{0,1:T(8,128)S(1)} %get-tuple-element.846), channel_id=1, source_target_pairs={{2,0},{3,1},{4,2},{5,3},{6,4},{7,5},{0,6},{1,7},{10,8},{11,9},{12,... | collective-permute-start | bytes 98312 | tf_op jit(solution)/shard_map/ppermute | solution.py:15
  22.0 29.3 %collective-permute-start.4 = (f32[64,128]{0,1:T(8,128)S(1)}, f32[64,128]{0,1:T(8,128)}, u32[]{:S(2)}, u32[]{:S(2)}) collective-permute-start(f32[64,128]{0,1:T(8,128)S(1)} %get-tuple-element.845), channel_id=1, source_target_pairs={{5,0},{6,1},{7,2},{0,3},{1,4},{2,5},{3,6},{4,7},{13,8},{14,9},{15,... | collective-permute-start | bytes 98312 | tf_op jit(solution)/shard_map/ppermute | solution.py:15
  42.2 10.5 %collective-permute-start.5 = (f32[64,128]{0,1:T(8,128)S(1)}, f32[64,128]{0,1:T(8,128)S(1)}, u32[]{:S(2)}, u32[]{:S(2)}) collective-permute-start(f32[64,128]{0,1:T(8,128)S(1)} %get-tuple-element.844), channel_id=1, source_target_pairs={{3,0},{4,1},{5,2},{6,3},{7,4},{0,5},{1,6},{2,7},{11,8},{12,9},{13,... | collective-permute-start | bytes 98312 | tf_op jit(solution)/shard_map/ppermute | solution.py:15
  168.2 72.6 %copy-start.4 = (f32[32,1024]{0,1:T(8,128)}, f32[32,1024]{0,1:T(8,128)S(1)}, u32[]{:S(2)}) copy-start(f32[32,1024]{0,1:T(8,128)S(1)} %get-tuple-element.832) | copy-start | bytes 393220
  169.5 22.9 %collective-permute-start.6 = (f32[32,128]{1,0:T(8,128)S(1)}, f32[32,128]{1,0:T(8,128)S(1)}, u32[]{:S(2)}, u32[]{:S(2)}) collective-permute-start(f32[32,128]{1,0:T(8,128)S(1)} %bitcast.325), channel_id=1, source_target_pairs={{7,0},{0,1},{1,2},{2,3},{3,4},{4,5},{5,6},{6,7},{15,8},{8,9},{9,10... | collective-permute-start | bytes 49160 | tf_op jit(solution)/shard_map/ppermute | solution.py:15
  169.5 26.1 %collective-permute-start.7 = (f32[32,128]{1,0:T(8,128)S(1)}, f32[32,128]{1,0:T(8,128)S(1)}, u32[]{:S(2)}, u32[]{:S(2)}) collective-permute-start(f32[32,128]{1,0:T(8,128)S(1)} %bitcast.319), channel_id=1, source_target_pairs={{1,0},{2,1},{3,2},{4,3},{5,4},{6,5},{7,6},{0,7},{9,8},{10,9},{11,1... | collective-permute-start | bytes 49160 | tf_op jit(solution)/shard_map/ppermute | solution.py:15
  174.9 21.3 %collective-permute-start.8 = (f32[32,128]{1,0:T(8,128)S(1)}, f32[32,128]{1,0:T(8,128)S(1)}, u32[]{:S(2)}, u32[]{:S(2)}) collective-permute-start(f32[32,128]{1,0:T(8,128)S(1)} %bitcast.315), channel_id=1, source_target_pairs={{6,0},{7,1},{0,2},{1,3},{2,4},{3,5},{4,6},{5,7},{14,8},{15,9},{8,1... | collective-permute-start | bytes 49160 | tf_op jit(solution)/shard_map/ppermute | solution.py:15
  174.9 22.0 %collective-permute-start.9 = (f32[32,128]{1,0:T(8,128)S(1)}, f32[32,128]{1,0:T(8,128)S(1)}, u32[]{:S(2)}, u32[]{:S(2)}) collective-permute-start(f32[32,128]{1,0:T(8,128)S(1)} %bitcast.311), channel_id=1, source_target_pairs={{2,0},{3,1},{4,2},{5,3},{6,4},{7,5},{0,6},{1,7},{10,8},{11,9},{12,... | collective-permute-start | bytes 49160 | tf_op jit(solution)/shard_map/ppermute | solution.py:15
  178.7 18.8 %collective-permute-start.10 = (f32[32,128]{1,0:T(8,128)S(1)}, f32[32,128]{1,0:T(8,128)S(1)}, u32[]{:S(2)}, u32[]{:S(2)}) collective-permute-start(f32[32,128]{1,0:T(8,128)S(1)} %bitcast.307), channel_id=1, source_target_pairs={{5,0},{6,1},{7,2},{0,3},{1,4},{2,5},{3,6},{4,7},{13,8},{14,9},{15,... | collective-permute-start | bytes 49160 | tf_op jit(solution)/shard_map/ppermute | solution.py:15
  192.4 5.7 collective-permute-start.11
  199.3 18.2 %copy-start.12 = (f32[8,384]{1,0:T(8,128)S(1)}, f32[8,384]{1,0:T(8,128)}, u32[]{:S(2)}) copy-start(f32[8,384]{1,0:T(8,128)} %mul.242) | copy-start | bytes 36868
  242.6 13.0 %collective-permute-start.12 = (f32[32,128]{1,0:T(8,128)S(1)}, f32[32,128]{1,0:T(8,128)S(1)}, u32[]{:S(2)}, u32[]{:S(2)}) collective-permute-start(f32[32,128]{1,0:T(8,128)S(1)} %bitcast.327), channel_id=1, source_target_pairs={{7,0},{0,1},{1,2},{2,3},{3,4},{4,5},{5,6},{6,7},{15,8},{8,9},{9,10... | collective-permute-start | bytes 49160 | tf_op jit(solution)/shard_map/ppermute | solution.py:15
  242.7 15.8 %collective-permute-start.13 = (f32[32,128]{1,0:T(8,128)S(1)}, f32[32,128]{1,0:T(8,128)S(1)}, u32[]{:S(2)}, u32[]{:S(2)}) collective-permute-start(f32[32,128]{1,0:T(8,128)S(1)} %bitcast.323), channel_id=1, source_target_pairs={{1,0},{2,1},{3,2},{4,3},{5,4},{6,5},{7,6},{0,7},{9,8},{10,9},{11,1... | collective-permute-start | bytes 49160 | tf_op jit(solution)/shard_map/ppermute | solution.py:15
  246.2 12.2 %collective-permute-start.14 = (f32[32,128]{1,0:T(8,128)S(1)}, f32[32,128]{1,0:T(8,128)S(1)}, u32[]{:S(2)}, u32[]{:S(2)}) collective-permute-start(f32[32,128]{1,0:T(8,128)S(1)} %bitcast.320), channel_id=1, source_target_pairs={{6,0},{7,1},{0,2},{1,3},{2,4},{3,5},{4,6},{5,7},{14,8},{15,9},{8,1... | collective-permute-start | bytes 49160 | tf_op jit(solution)/shard_map/ppermute | solution.py:15
  246.2 12.2 %collective-permute-start.15 = (f32[32,128]{1,0:T(8,128)S(1)}, f32[32,128]{1,0:T(8,128)S(1)}, u32[]{:S(2)}, u32[]{:S(2)}) collective-permute-start(f32[32,128]{1,0:T(8,128)S(1)} %bitcast.316), channel_id=1, source_target_pairs={{2,0},{3,1},{4,2},{5,3},{6,4},{7,5},{0,6},{1,7},{10,8},{11,9},{12,... | collective-permute-start | bytes 49160 | tf_op jit(solution)/shard_map/ppermute | solution.py:15
  250.1 8.4 %collective-permute-start.16 = (f32[32,128]{1,0:T(8,128)S(1)}, f32[32,128]{1,0:T(8,128)S(1)}, u32[]{:S(2)}, u32[]{:S(2)}) collective-permute-start(f32[32,128]{1,0:T(8,128)S(1)} %bitcast.312), channel_id=1, source_target_pairs={{5,0},{6,1},{7,2},{0,3},{1,4},{2,5},{3,6},{4,7},{13,8},{14,9},{15,... | collective-permute-start | bytes 49160 | tf_op jit(solution)/shard_map/ppermute | solution.py:15
  255.6 4.3 collective-permute-start.17
  294.8 126.6 %copy-start = (f32[32,1024]{0,1:T(8,128)}, f32[32,1024]{0,1:T(8,128)S(1)}, u32[]{:S(2)}) copy-start(f32[32,1024]{0,1:T(8,128)S(1)} %get-tuple-element.830) | copy-start | bytes 393220
  314.5 14.0 %collective-permute-start.18 = (f32[64,128]{0,1:T(8,128)S(1)}, f32[64,128]{0,1:T(8,128)S(1)}, u32[]{:S(2)}, u32[]{:S(2)}) collective-permute-start(f32[64,128]{0,1:T(8,128)S(1)} %get-tuple-element.843), channel_id=1, source_target_pairs={{7,0},{0,1},{1,2},{2,3},{3,4},{4,5},{5,6},{6,7},{15,8},{8,9},{9,10... | collective-permute-start | bytes 98312 | tf_op jit(solution)/shard_map/ppermute | solution.py:15
  315.6 16.2 %collective-permute-start.19 = (f32[64,128]{0,1:T(8,128)S(1)}, f32[64,128]{0,1:T(8,128)S(1)}, u32[]{:S(2)}, u32[]{:S(2)}) collective-permute-start(f32[64,128]{0,1:T(8,128)S(1)} %get-tuple-element.842), channel_id=1, source_target_pairs={{1,0},{2,1},{3,2},{4,3},{5,4},{6,5},{7,6},{0,7},{9,8},{10,9},{11,1... | collective-permute-start | bytes 98312 | tf_op jit(solution)/shard_map/ppermute | solution.py:15
  319.1 13.2 %collective-permute-start.20 = (f32[64,128]{0,1:T(8,128)S(1)}, f32[64,128]{0,1:T(8,128)S(1)}, u32[]{:S(2)}, u32[]{:S(2)}) collective-permute-start(f32[64,128]{0,1:T(8,128)S(1)} %get-tuple-element.841), channel_id=1, source_target_pairs={{6,0},{7,1},{0,2},{1,3},{2,4},{3,5},{4,6},{5,7},{14,8},{15,9},{8,1... | collective-permute-start | bytes 98312 | tf_op jit(solution)/shard_map/ppermute | solution.py:15
  319.2 13.9 %collective-permute-start.21 = (f32[64,128]{0,1:T(8,128)S(1)}, f32[64,128]{0,1:T(8,128)S(1)}, u32[]{:S(2)}, u32[]{:S(2)}) collective-permute-start(f32[64,128]{0,1:T(8,128)S(1)} %get-tuple-element.840), channel_id=1, source_target_pairs={{2,0},{3,1},{4,2},{5,3},{6,4},{7,5},{0,6},{1,7},{10,8},{11,9},{12,... | collective-permute-start | bytes 98312 | tf_op jit(solution)/shard_map/ppermute | solution.py:15
  323.0 10.7 %collective-permute-start.22 = (f32[64,128]{0,1:T(8,128)S(1)}, f32[64,128]{0,1:T(8,128)S(1)}, u32[]{:S(2)}, u32[]{:S(2)}) collective-permute-start(f32[64,128]{0,1:T(8,128)S(1)} %get-tuple-element.839), channel_id=1, source_target_pairs={{5,0},{6,1},{7,2},{0,3},{1,4},{2,5},{3,6},{4,7},{13,8},{14,9},{15,... | collective-permute-start | bytes 98312 | tf_op jit(solution)/shard_map/ppermute | solution.py:15
  328.5 5.8 collective-permute-start.23
  341.4 17.1 %copy-start.11 = (f32[32,3072]{1,0:T(8,128)S(1)}, f32[32,3072]{1,0:T(8,128)}, u32[]{:S(2)}) copy-start(f32[32,3072]{1,0:T(8,128)} %param.48) | copy-start | bytes 1179652
  341.5 17.1 %copy-start.24 = (f32[3072]{0:T(1024)S(1)}, f32[3072]{0:T(1024)}, u32[]{:S(2)}) copy-start(f32[3072]{0:T(1024)} %param.49) | copy-start | bytes 36868
  382.9 10.8 %copy-start.13 = (f32[8,384]{1,0:T(8,128)S(1)}, f32[8,384]{1,0:T(8,128)}, u32[]{:S(2)}) copy-start(f32[8,384]{1,0:T(8,128)} %mul.242) | copy-start | bytes 36868
  426.4 12.2 %collective-permute-start.24 = (f32[32,128]{1,0:T(8,128)S(1)}, f32[32,128]{1,0:T(8,128)}, u32[]{:S(2)}, u32[]{:S(2)}) collective-permute-start(f32[32,128]{1,0:T(8,128)S(1)} %bitcast.326), channel_id=1, source_target_pairs={{7,0},{0,1},{1,2},{2,3},{3,4},{4,5},{5,6},{6,7},{15,8},{8,9},{9,10... | collective-permute-start | bytes 49160 | tf_op jit(solution)/shard_map/ppermute | solution.py:15
  427.1 14.8 %collective-permute-start.25 = (f32[32,128]{1,0:T(8,128)S(1)}, f32[32,128]{1,0:T(8,128)}, u32[]{:S(2)}, u32[]{:S(2)}) collective-permute-start(f32[32,128]{1,0:T(8,128)S(1)} %bitcast.322), channel_id=1, source_target_pairs={{1,0},{2,1},{3,2},{4,3},{5,4},{6,5},{7,6},{0,7},{9,8},{10,9},{11,1... | collective-permute-start | bytes 49160 | tf_op jit(solution)/shard_map/ppermute | solution.py:15
  430.7 12.0 %collective-permute-start.26 = (f32[32,128]{1,0:T(8,128)S(1)}, f32[32,128]{1,0:T(8,128)}, u32[]{:S(2)}, u32[]{:S(2)}) collective-permute-start(f32[32,128]{1,0:T(8,128)S(1)} %bitcast.318), channel_id=1, source_target_pairs={{6,0},{7,1},{0,2},{1,3},{2,4},{3,5},{4,6},{5,7},{14,8},{15,9},{8,1... | collective-permute-start | bytes 49160 | tf_op jit(solution)/shard_map/ppermute | solution.py:15
  430.7 12.7 %collective-permute-start.27 = (f32[32,128]{1,0:T(8,128)S(1)}, f32[32,128]{1,0:T(8,128)S(1)}, u32[]{:S(2)}, u32[]{:S(2)}) collective-permute-start(f32[32,128]{1,0:T(8,128)S(1)} %bitcast.314), channel_id=1, source_target_pairs={{2,0},{3,1},{4,2},{5,3},{6,4},{7,5},{0,6},{1,7},{10,8},{11,9},{12,... | collective-permute-start | bytes 49160 | tf_op jit(solution)/shard_map/ppermute | solution.py:15
  434.5 8.9 %collective-permute-start.28 = (f32[32,128]{1,0:T(8,128)S(1)}, f32[32,128]{1,0:T(8,128)S(1)}, u32[]{:S(2)}, u32[]{:S(2)}) collective-permute-start(f32[32,128]{1,0:T(8,128)S(1)} %bitcast.310), channel_id=1, source_target_pairs={{5,0},{6,1},{7,2},{0,3},{1,4},{2,5},{3,6},{4,7},{13,8},{14,9},{15,... | collective-permute-start | bytes 49160 | tf_op jit(solution)/shard_map/ppermute | solution.py:15
  438.6 4.8 collective-permute-start.29
  475.7 13.0 %collective-permute-start.30 = (f32[32,128]{1,0:T(8,128)S(1)}, f32[32,128]{1,0:T(8,128)S(1)}, u32[]{:S(2)}, u32[]{:S(2)}) collective-permute-start(f32[32,128]{1,0:T(8,128)S(1)} %bitcast.328), channel_id=1, source_target_pairs={{7,0},{0,1},{1,2},{2,3},{3,4},{4,5},{5,6},{6,7},{15,8},{8,9},{9,10... | collective-permute-start | bytes 49160 | tf_op jit(solution)/shard_map/ppermute | solution.py:15
  475.8 15.8 %collective-permute-start.31 = (f32[32,128]{1,0:T(8,128)S(1)}, f32[32,128]{1,0:T(8,128)S(1)}, u32[]{:S(2)}, u32[]{:S(2)}) collective-permute-start(f32[32,128]{1,0:T(8,128)S(1)} %bitcast.324), channel_id=1, source_target_pairs={{1,0},{2,1},{3,2},{4,3},{5,4},{6,5},{7,6},{0,7},{9,8},{10,9},{11,1... | collective-permute-start | bytes 49160 | tf_op jit(solution)/shard_map/ppermute | solution.py:15
  479.3 12.2 %collective-permute-start.32 = (f32[32,128]{1,0:T(8,128)S(1)}, f32[32,128]{1,0:T(8,128)S(1)}, u32[]{:S(2)}, u32[]{:S(2)}) collective-permute-start(f32[32,128]{1,0:T(8,128)S(1)} %bitcast.321), channel_id=1, source_target_pairs={{6,0},{7,1},{0,2},{1,3},{2,4},{3,5},{4,6},{5,7},{14,8},{15,9},{8,1... | collective-permute-start | bytes 49160 | tf_op jit(solution)/shard_map/ppermute | solution.py:15
  479.3 12.2 %collective-permute-start.33 = (f32[32,128]{1,0:T(8,128)S(1)}, f32[32,128]{1,0:T(8,128)S(1)}, u32[]{:S(2)}, u32[]{:S(2)}) collective-permute-start(f32[32,128]{1,0:T(8,128)S(1)} %bitcast.317), channel_id=1, source_target_pairs={{2,0},{3,1},{4,2},{5,3},{6,4},{7,5},{0,6},{1,7},{10,8},{11,9},{12,... | collective-permute-start | bytes 49160 | tf_op jit(solution)/shard_map/ppermute | solution.py:15
  483.2 8.4 %collective-permute-start.34 = (f32[32,128]{1,0:T(8,128)S(1)}, f32[32,128]{1,0:T(8,128)S(1)}, u32[]{:S(2)}, u32[]{:S(2)}) collective-permute-start(f32[32,128]{1,0:T(8,128)S(1)} %bitcast.313), channel_id=1, source_target_pairs={{5,0},{6,1},{7,2},{0,3},{1,4},{2,5},{3,6},{4,7},{13,8},{14,9},{15,... | collective-permute-start | bytes 49160 | tf_op jit(solution)/shard_map/ppermute | solution.py:15
  488.7 4.3 collective-permute-start.35
  (32 other events, 162.2 us)
Sparse Core Ops, SparseCore 0:
  557.9 44.0 all-reduce.6
where the time goes:
time: 620 us; the launch traced here: 611 us
  matrix products  185 us (30%)
  local copies, waits for them, and re-layouts  175 us (28%)
  other arithmetic  93.5 us (15%)
  starting transfers between devices  62.6 us (10%)
  waiting for transfers between devices  46 us (7%)
  blocking collectives  29 us (5%)
  between operations  17.2 us (3%)
    dot_general x132, matrix products, exact_dot(): jnp.dot(left_side, right_side, precision=lax.Precision.HIGHEST, preferred...  179 us
    ppermute x36, starting transfers between devices, passed_along(): return lax.ppermute(block, axis, route)  62.5 us
    reduce_sum x8, other arithmetic, divergence(): outgoing = jnp.sum(fluxes.reshape(levels, cell_count, 3), axis=2)  50.5 us
    psum x1, waiting for transfers between devices, per_device(): ensemble = lax.psum(current, 'member') / lax.axis_size('member')  43.2 us
    unnamed x140, local copies, waits for them, and re-layouts  39.7 us
    reshape x10, local copies, waits for them, and re-layouts, starts_of(): jnp.broadcast_to(fields[:, :, None], (levels, cell_count, 3))  31.1 us
    psum x2, blocking collectives, per_device(): lax.psum((jnp.sum(current * cell_area[None, :], axis=1), jnp.sum(cell_are...  29 us
    transpose x6, other arithmetic, divergence(): jnp.transpose(fluxes.reshape(levels, block_count, block_size), (1, 0, 2))  19.8 us
  transfers between devices with their start and end apart: 37, of which 3 were waited for; matrix products, arithmetic and copies ran while one was open for 12% of the time, Pallas kernels for 0%

commit v1 on v0

--- a/solution.py
+++ b/solution.py
@@ -169,7 +169,7 @@
         current = jnp.where(owned, current - level_mean, current)
         previous = jnp.where(owned, previous - level_mean, previous)
         scalar_quantity = advanced
-    ensemble = lax.psum(current, "member") / lax.axis_size("member")
+    ensemble = jnp.sum(lax.all_gather(current, "member"), axis=0) / lax.axis_size("member")
     return (current[None], scalar_quantity[None], ensemble)
 
 

time: 620 us -> 572 us (0.923)
  waiting for transfers between devices: 46 us -> 2.82 us
  between operations: 17.2 us -> 3.76 us
  blocking collectives: 29 us -> 39.6 us
    psum x1 -> x0, waiting for transfers between devices: 43.2 us -> none  [per_device(): ensemble = lax.psum(current, 'member') / lax.axis_size('member')]
    all_gather x0 -> x1, blocking collectives: none -> 10.5 us  [per_device(): lax.all_gather(current, 'member')]
  transfers between devices with their start and end apart: 37 -> 36, of which waited for: 3 -> 2; matrix products, arithmetic and copies ran while one was open for 12% -> 13% of each run, Pallas kernels for 0% -> 0%
where the time goes in v1:
time: 572 us; the launch traced here: 563 us
  matrix products  185 us (32%)
  local copies, waits for them, and re-layouts  175 us (31%)
  other arithmetic  91.4 us (16%)
  starting transfers between devices  62.5 us (11%)
  blocking collectives  39.6 us (7%)
    dot_general x132, matrix products, exact_dot(): jnp.dot(left_side, right_side, precision=lax.Precision.HIGHEST, preferred...  179 us
    ppermute x36, starting transfers between devices, passed_along(): return lax.ppermute(block, axis, route)  62.5 us
    reduce_sum x8, other arithmetic, divergence(): outgoing = jnp.sum(fluxes.reshape(levels, cell_count, 3), axis=2)  50.5 us
    unnamed x140, local copies, waits for them, and re-layouts  39.7 us
    reshape x10, local copies, waits for them, and re-layouts, starts_of(): jnp.broadcast_to(fields[:, :, None], (levels, cell_count, 3))  31.2 us
    psum x2, blocking collectives, per_device(): lax.psum((jnp.sum(current * cell_area[None, :], axis=1), jnp.sum(cell_are...  29 us
    transpose x6, other arithmetic, divergence(): jnp.transpose(fluxes.reshape(levels, block_count, block_size), (1, 0, 2))  19.9 us
    dynamic_slice x16, local copies, waits for them, and re-layouts, divergence(): lax.scan(add_block, jnp.zeros((levels, cell_count), jnp.float32), (index_...  16.5 us
  transfers between devices with their start and end apart: 36, of which 2 were waited for; matrix products, arithmetic and copies ran while one was open for 13% of the time, Pallas kernels for 0%

profile of v1, /device:TPU:0, one launch (start us, length us, event | category | flops | bytes accessed | tf_op | source)
XLA Modules:
  0.0 562.9 jit_solution(16956031343688051882)
XLA Ops:
  7.6 4.0 collective-permute-start.1
  24.0 3.8 reshape.204
  51.6 9.1 %while.168 = (s32[]{:T(128)}, f32[8,32,384]{2,1,0:T(8,128)S(1)}, s32[8,384]{1,0:T(8,128)S(1)}, f32[32,1793]{1,0:T(8,128)S(1)}, s32[]{:T(128)}) while((s32[]{:T(128)}, f32[8,32,384]{2,1,0:T(8,128)S(1)}, s32[8,384]{1,0:T(8,128)S(1)}, f32[32,1793]{1,0:T(8,128)S(1)}, s32[]{:T(128)}) %tuple.362), condition=%wide.region_1.2_spmd, body=%wide.region_0.1_spmd.sunk | while | flops 265077120 | bytes 300101 | solution.py:44
  66.0 22.9 %while.176 = (s32[]{:T(128)}, f32[32,1024]{1,0:T(8,128)}, f32[8,32,384]{2,1,0:T(8,128)S(1)}, s32[8,384]{1,0:T(8,128)S(1)}, s32[]{:T(128)}, /*index=5*/s32[]{:T(128)}) while((s32[]{:T(128)}, f32[32,1024]{1,0:T(8,128)}, f32[8,32,384]{2,1,0:T(8,128)S(1)}, s32[8,384]{1,0:T(8,128)S(1)}, s32[]{:T(128)}, /*index=5*/s32[]{:T(128)}) %tuple.410), condition=%wide.region_4.5_spmd.clone, body=%wide.region_3.4_spmd.clone.sunk | while | flops 151453696 | bytes 315991 | solution.py:63
  93.1 16.6 %while.169 = (s32[]{:T(128)}, f32[8,32,384]{2,1,0:T(8,128)S(1)}, s32[8,384]{1,0:T(8,128)S(1)}, f32[32,1793]{1,0:T(8,128)}, s32[]{:T(128)}) while((s32[]{:T(128)}, f32[8,32,384]{2,1,0:T(8,128)S(1)}, s32[8,384]{1,0:T(8,128)S(1)}, f32[32,1793]{1,0:T(8,128)}, s32[]{:T(128)}) %tuple.411), condition=%wide.region_6.7_spmd, body=%wide.region_5.6_spmd.sunk | while | flops 265077120 | bytes 283845 | solution.py:44
  113.5 25.9 %while.177 = (s32[]{:T(128)}, f32[32,1024]{1,0:T(8,128)}, f32[8,32,384]{2,0,1:T(8,128)}, s32[8,384]{1,0:T(8,128)S(1)}, s32[]{:T(128)}, /*index=5*/s32[]{:T(128)}) while((s32[]{:T(128)}, f32[32,1024]{1,0:T(8,128)}, f32[8,32,384]{2,0,1:T(8,128)}, s32[8,384]{1,0:T(8,128)S(1)}, s32[]{:T(128)}, /*index=5*/s32[]{:T(128)}) %tuple.425), condition=%wide.region_9.10_spmd.clone, body=%wide.region_8.9_spmd.clone.sunk | while | flops 151453696 | bytes 414295 | solution.py:63
  143.0 3.7 reshape.207
  146.6 7.7 %multiply_reduce_fusion.5 = f32[32,1024]{0,1:T(8,128)} fusion(f32[32,1024,3]{0,2,1:T(4,128)} %reshape.203, f32[32,1024]{0,1:T(8,128)S(1)} %bitcast.285, f32[1024,3]{1,0:T(8,128)S(1)} %mul.239), kind=kLoop, calls=%fused_computation.122 | loop fusion | flops 262144 | bytes 667648 | tf_op jit(solution)/shard_map/reduce_sum | solution.py:66
  154.3 3.7 reduce_sum.113
  162.6 3.7 collective-permute-start.7
  168.0 3.8 collective-permute-start.9
  173.5 3.8 reshape.211
  179.1 3.8 reshape.218
  192.4 16.6 %while.170 = (s32[]{:T(128)}, f32[8,32,384]{2,1,0:T(8,128)S(1)}, s32[8,384]{1,0:T(8,128)S(1)}, f32[32,1793]{1,0:T(8,128)}, s32[]{:T(128)}) while((s32[]{:T(128)}, f32[8,32,384]{2,1,0:T(8,128)S(1)}, s32[8,384]{1,0:T(8,128)S(1)}, f32[32,1793]{1,0:T(8,128)}, s32[]{:T(128)}) %tuple.413), condition=%wide.region_11.12_spmd, body=%wide.region_10.11_spmd.sunk | while | flops 265077120 | bytes 283845 | solution.py:44
  216.1 6.2 %while.178 = (s32[]{:T(128)}, f32[32,1024]{1,0:T(8,128)S(1)}, f32[8,32,384]{2,1,0:T(8,128)S(1)}, s32[8,384]{1,0:T(8,128)S(1)}, s32[]{:T(128)}, /*index=5*/s32[]{:T(128)}) while((s32[]{:T(128)}, f32[32,1024]{1,0:T(8,128)S(1)}, f32[8,32,384]{2,1,0:T(8,128)S(1)}, s32[8,384]{1,0:T(8,128)S(1)}, s32[]{:T(128)}, ...), condition=%wide.region_14.15_spmd.clone, body=%wide.region_13.14_spmd.clone.sunk | while | flops 151453696 | bytes 316503 | solution.py:63
  223.3 3.7 reshape.210
  227.0 6.9 %multiply_reduce_fusion.4 = f32[32,1024]{0,1:T(8,128)S(1)} fusion(f32[32,1024,3]{0,2,1:T(4,128)} %reshape.210, f32[32,1024]{0,1:T(8,128)S(1)} %get-tuple-element.898, f32[1024,3]{1,0:T(8,128)S(1)} %mul.239), kind=kLoop, calls=%fused_computation.121 | loop fusion | flops 262144 | bytes 667648 | tf_op jit(solution)/shard_map/reduce_sum | solution.py:66
  235.7 3.6 collective-permute-start.13
  239.3 3.8 collective-permute-start.15
  244.8 3.8 reshape.214
  253.0 9.0 %while.171 = (s32[]{:T(128)}, f32[8,32,384]{2,1,0:T(8,128)S(1)}, s32[8,384]{1,0:T(8,128)S(1)}, f32[32,1793]{1,0:T(8,128)S(1)}, s32[]{:T(128)}) while((s32[]{:T(128)}, f32[8,32,384]{2,1,0:T(8,128)S(1)}, s32[8,384]{1,0:T(8,128)S(1)}, f32[32,1793]{1,0:T(8,128)S(1)}, s32[]{:T(128)}) %tuple.415), condition=%wide.region_16.17_spmd, body=%wide.region_15.16_spmd.sunk | while | flops 265077120 | bytes 300101 | solution.py:44
  269.1 6.2 %while.179 = (s32[]{:T(128)}, f32[32,1024]{1,0:T(8,128)S(1)}, f32[8,32,384]{2,1,0:T(8,128)S(1)}, s32[8,384]{1,0:T(8,128)S(1)}, s32[]{:T(128)}, /*index=5*/s32[]{:T(128)}) while((s32[]{:T(128)}, f32[32,1024]{1,0:T(8,128)S(1)}, f32[8,32,384]{2,1,0:T(8,128)S(1)}, s32[8,384]{1,0:T(8,128)S(1)}, s32[]{:T(128)}, ...), condition=%wide.region_19.20_spmd.clone, body=%wide.region_18.19_spmd.clone.sunk | while | flops 151453696 | bytes 316503 | solution.py:63
  276.3 3.7 reshape.213
  280.0 6.9 %multiply_reduce_fusion.3 = f32[32,1024]{0,1:T(8,128)S(1)} fusion(f32[32,1024,3]{0,2,1:T(4,128)} %reshape.213, f32[32,1024]{0,1:T(8,128)S(1)} %add_select_fusion.5, f32[1024,3]{1,0:T(8,128)S(1)} %mul.239), kind=kLoop, calls=%fused_computation.120 | loop fusion | flops 262144 | bytes 667648 | tf_op jit(solution)/shard_map/reduce_sum | solution.py:66
  287.9 14.8 %all-reduce.4 = (f32[32]{0:T(128)S(1)}, f32[]{:T(128)}) all-reduce(f32[32]{0:T(128)S(1)} %get-tuple-element.896, f32[]{:T(128)} %get-tuple-element.943), channel_id=1, replica_groups=mesh['member'=4,'dom'=8] {'dom'}, use_global_device_ids=true, to_apply=%region_21.22 | all-reduce | flops 33 | bytes 264 | tf_op jit(solution)/shard_map/psum | solution.py:165
  312.2 3.8 collective-permute-start.21
  317.7 3.8 reshape.217
  334.6 17.0 %while.173 = (s32[]{:T(128)}, f32[8,32,384]{2,1,0:T(8,128)S(1)}, s32[8,384]{1,0:T(8,128)S(1)}, f32[32,1793]{1,0:T(8,128)}, s32[]{:T(128)}) while((s32[]{:T(128)}, f32[8,32,384]{2,1,0:T(8,128)S(1)}, s32[8,384]{1,0:T(8,128)S(1)}, f32[32,1793]{1,0:T(8,128)}, s32[]{:T(128)}) %tuple.417), condition=%wide.region_30.31_spmd, body=%wide.region_29.30_spmd.sunk | while | flops 265077120 | bytes 283845 | solution.py:44
  354.4 3.7 reshape.220
  358.9 14.6 %while.181 = (s32[]{:T(128)}, f32[32,1024]{1,0:T(8,128)S(1)}, f32[8,32,384]{2,0,1:T(8,128)}, s32[8,384]{1,0:T(8,128)S(1)}, s32[]{:T(128)}, /*index=5*/s32[]{:T(128)}) while((s32[]{:T(128)}, f32[32,1024]{1,0:T(8,128)S(1)}, f32[8,32,384]{2,0,1:T(8,128)}, s32[8,384]{1,0:T(8,128)S(1)}, s32[]{:T(128)}, /*index=5*/s32[]{:T(128)}) %tuple.429), condition=%wide.region_33.34_spmd.clone, body=%wide.region_32.33_spmd.clone.sunk | while | flops 151453696 | bytes 414295 | solution.py:63
  376.0 9.1 %while.172 = (s32[]{:T(128)}, f32[8,32,384]{2,1,0:T(8,128)S(1)}, s32[8,384]{1,0:T(8,128)S(1)}, f32[32,1793]{1,0:T(8,128)S(1)}, s32[]{:T(128)}) while((s32[]{:T(128)}, f32[8,32,384]{2,1,0:T(8,128)S(1)}, s32[8,384]{1,0:T(8,128)S(1)}, f32[32,1793]{1,0:T(8,128)S(1)}, s32[]{:T(128)}) %tuple.419), condition=%wide.region_25.26_spmd, body=%wide.region_24.25_spmd.sunk | while | flops 265077120 | bytes 300101 | solution.py:44
  392.2 6.2 %while.180 = (s32[]{:T(128)}, f32[32,1024]{1,0:T(8,128)S(1)}, f32[8,32,384]{2,1,0:T(8,128)S(1)}, s32[8,384]{1,0:T(8,128)S(1)}, s32[]{:T(128)}, /*index=5*/s32[]{:T(128)}) while((s32[]{:T(128)}, f32[32,1024]{1,0:T(8,128)S(1)}, f32[8,32,384]{2,1,0:T(8,128)S(1)}, s32[8,384]{1,0:T(8,128)S(1)}, s32[]{:T(128)}, ...), condition=%wide.region_28.29_spmd.clone, body=%wide.region_27.28_spmd.clone.sunk | while | flops 151453696 | bytes 316503 | solution.py:63
  399.5 3.6 reshape.216
  403.1 7.7 %multiply_reduce_fusion.2 = f32[32,1024]{0,1:T(8,128)} fusion(f32[32,1024,3]{0,2,1:T(4,128)} %reshape.216, f32[32,1024]{0,1:T(8,128)S(1)} %subtract_select_fusion.2, f32[1024,3]{1,0:T(8,128)S(1)} %mul.239), kind=kLoop, calls=%fused_computation.119 | loop fusion | flops 262144 | bytes 667648 | tf_op jit(solution)/shard_map/reduce_sum | solution.py:66
  410.8 3.7 reduce_sum.119
  414.5 3.6 fusion.89
  423.7 3.8 collective-permute-start.27
  436.5 9.1 %while.174 = (s32[]{:T(128)}, f32[8,32,384]{2,1,0:T(8,128)S(1)}, s32[8,384]{1,0:T(8,128)S(1)}, f32[32,1793]{1,0:T(8,128)S(1)}, s32[]{:T(128)}) while((s32[]{:T(128)}, f32[8,32,384]{2,1,0:T(8,128)S(1)}, s32[8,384]{1,0:T(8,128)S(1)}, f32[32,1793]{1,0:T(8,128)S(1)}, s32[]{:T(128)}) %tuple.421), condition=%wide.region_35.36_spmd, body=%wide.region_34.35_spmd.sunk | while | flops 265077120 | bytes 300101 | solution.py:44
  451.0 6.2 %while.182 = (s32[]{:T(128)}, f32[32,1024]{1,0:T(8,128)S(1)}, f32[8,32,384]{2,1,0:T(8,128)S(1)}, s32[8,384]{1,0:T(8,128)S(1)}, s32[]{:T(128)}, /*index=5*/s32[]{:T(128)}) while((s32[]{:T(128)}, f32[32,1024]{1,0:T(8,128)S(1)}, f32[8,32,384]{2,1,0:T(8,128)S(1)}, s32[8,384]{1,0:T(8,128)S(1)}, s32[]{:T(128)}, ...), condition=%wide.region_38.39_spmd.clone, body=%wide.region_37.38_spmd.clone.sunk | while | flops 151453696 | bytes 316503 | solution.py:63
  459.9 7.0 %multiply_reduce_fusion.1 = f32[32,1024]{0,1:T(8,128)S(1)} fusion(f32[32,1024,3]{0,2,1:T(4,128)} %reshape.223, f32[32,1024]{0,1:T(8,128)S(1)} %get-tuple-element.891, f32[1024,3]{1,0:T(8,128)S(1)} %mul.239), kind=kLoop, calls=%fused_computation.118 | loop fusion | flops 262144 | bytes 667648 | tf_op jit(solution)/shard_map/reduce_sum | solution.py:66
  468.7 3.6 collective-permute-start.31
  472.3 3.8 collective-permute-start.33
  477.9 3.8 reshape.227
  486.0 9.0 %while.175 = (s32[]{:T(128)}, f32[8,32,384]{2,1,0:T(8,128)S(1)}, s32[8,384]{1,0:T(8,128)S(1)}, f32[32,1793]{1,0:T(8,128)S(1)}, s32[]{:T(128)}) while((s32[]{:T(128)}, f32[8,32,384]{2,1,0:T(8,128)S(1)}, s32[8,384]{1,0:T(8,128)S(1)}, f32[32,1793]{1,0:T(8,128)S(1)}, s32[]{:T(128)}) %tuple.423), condition=%wide.region_40.41_spmd, body=%wide.region_39.40_spmd.sunk | while | flops 265077120 | bytes 300101 | solution.py:44
  500.4 22.8 %while.183 = (s32[]{:T(128)}, f32[32,1024]{1,0:T(8,128)}, f32[8,32,384]{2,1,0:T(8,128)S(1)}, s32[8,384]{1,0:T(8,128)S(1)}, s32[]{:T(128)}, /*index=5*/s32[]{:T(128)}) while((s32[]{:T(128)}, f32[32,1024]{1,0:T(8,128)}, f32[8,32,384]{2,1,0:T(8,128)S(1)}, s32[8,384]{1,0:T(8,128)S(1)}, s32[]{:T(128)}, /*index=5*/s32[]{:T(128)}) %tuple.424), condition=%wide.region_43.44_spmd.clone, body=%wide.region_42.43_spmd.clone.sunk | while | flops 151453696 | bytes 315991 | solution.py:63
  526.8 6.9 %multiply_reduce_fusion = f32[32,1024]{0,1:T(8,128)S(1)} fusion(f32[32,1024,3]{0,2,1:T(4,128)} %reshape.226, f32[32,1024]{0,1:T(8,128)S(1)} %add_select_fusion.3, f32[1024,3]{1,0:T(8,128)S(1)} %mul.239), kind=kLoop, calls=%fused_computation.117 | loop fusion | flops 262144 | bytes 667648 | tf_op jit(solution)/shard_map/reduce_sum | solution.py:66
  534.7 14.2 %psum.26 = f32[32]{0:T(128)S(1)} all-reduce(f32[32]{0:T(128)S(1)} %get-tuple-element.889), channel_id=1, replica_groups=mesh['member'=4,'dom'=8] {'dom'}, use_global_device_ids=true, to_apply=%region_45.46 | all-reduce | flops 32 | bytes 256 | tf_op jit(solution)/shard_map/psum | solution.py:165
  550.1 10.5 %all-gather = f32[128,1024]{1,0:T(8,128)S(1)} all-gather(f32[32,1024]{1,0:T(8,128)S(1)} %copy.368), channel_id=2, replica_groups=mesh['member'=4,'dom'=8] {'member'}, dimensions={0}, use_global_device_ids=true | all-gather | bytes 655360 | tf_op jit(solution)/shard_map/all_gather | solution.py:172
  (591 shorter events, 387.2 us)
Async XLA Ops:
  3.6 12.9 %copy-start.35 = (s32[6,128]{1,0:T(8,128)}, s32[6,128]{1,0:T(8,128)S(1)}, u32[]{:S(2)}) copy-start(s32[6,128]{1,0:T(8,128)S(1)} %reduce.17) | copy-start | bytes 9220
  6.4 11.1 %copy-start.31 = (s32[2,3072]{1,0:T(2,128)S(1)}, s32[2,3072]{1,0:T(2,128)}, u32[]{:S(2)}) copy-start(s32[2,3072]{1,0:T(2,128)} %param.54) | copy-start | bytes 73732
  6.4 11.1 %copy-start.30 = (f32[1,4]{1,0:T(1,128)S(1)}, f32[1,4]{1,0:T(1,128)}, u32[]{:S(2)}) copy-start(f32[1,4]{1,0:T(1,128)} %param.47) | copy-start | bytes 52
  6.4 12.4 %copy-start.40 = (f32[1024]{0:T(1024)S(1)}, f32[1024]{0:T(1024)}, u32[]{:S(2)}) copy-start(f32[1024]{0:T(1024)} %param.51) | copy-start | bytes 12292
  6.4 14.9 %copy-start.25 = (f32[3072]{0:T(1024)S(1)}, f32[3072]{0:T(1024)}, u32[]{:S(2)}) copy-start(f32[3072]{0:T(1024)} %param.50) | copy-start | bytes 36868
  7.1 28.5 %collective-permute-start = (f32[64,128]{0,1:T(8,128)}, f32[64,128]{0,1:T(8,128)}, u32[]{:S(2)}, u32[]{:S(2)}) collective-permute-start(f32[64,128]{0,1:T(8,128)} %get-tuple-element.916), channel_id=1, source_target_pairs={{7,0},{0,1},{1,2},{2,3},{3,4},{4,5},{5,6},{6,7},{15,8},{8,9},{9,10... | collective-permute-start | bytes 98312 | tf_op jit(solution)/shard_map/ppermute | solution.py:15
  7.6 32.7 %collective-permute-start.1 = (f32[64,128]{0,1:T(8,128)}, f32[64,128]{0,1:T(8,128)}, u32[]{:S(2)}, u32[]{:S(2)}) collective-permute-start(f32[64,128]{0,1:T(8,128)} %get-tuple-element.915), channel_id=1, source_target_pairs={{1,0},{2,1},{3,2},{4,3},{5,4},{6,5},{7,6},{0,7},{9,8},{10,9},{11,1... | collective-permute-start | bytes 98312 | tf_op jit(solution)/shard_map/ppermute | solution.py:15
  11.6 30.1 %collective-permute-start.2 = (f32[64,128]{0,1:T(8,128)S(1)}, f32[64,128]{0,1:T(8,128)}, u32[]{:S(2)}, u32[]{:S(2)}) collective-permute-start(f32[64,128]{0,1:T(8,128)S(1)} %get-tuple-element.914), channel_id=1, source_target_pairs={{6,0},{7,1},{0,2},{1,3},{2,4},{3,5},{4,6},{5,7},{14,8},{15,9},{8,1... | collective-permute-start | bytes 98312 | tf_op jit(solution)/shard_map/ppermute | solution.py:15
  11.9 31.3 %collective-permute-start.3 = (f32[64,128]{0,1:T(8,128)S(1)}, f32[64,128]{0,1:T(8,128)}, u32[]{:S(2)}, u32[]{:S(2)}) collective-permute-start(f32[64,128]{0,1:T(8,128)S(1)} %get-tuple-element.913), channel_id=1, source_target_pairs={{2,0},{3,1},{4,2},{5,3},{6,4},{7,5},{0,6},{1,7},{10,8},{11,9},{12,... | collective-permute-start | bytes 98312 | tf_op jit(solution)/shard_map/ppermute | solution.py:15
  15.4 29.3 %collective-permute-start.4 = (f32[64,128]{0,1:T(8,128)S(1)}, f32[64,128]{0,1:T(8,128)}, u32[]{:S(2)}, u32[]{:S(2)}) collective-permute-start(f32[64,128]{0,1:T(8,128)S(1)} %get-tuple-element.912), channel_id=1, source_target_pairs={{5,0},{6,1},{7,2},{0,3},{1,4},{2,5},{3,6},{4,7},{13,8},{14,9},{15,... | collective-permute-start | bytes 98312 | tf_op jit(solution)/shard_map/ppermute | solution.py:15
  35.6 10.5 %collective-permute-start.5 = (f32[64,128]{0,1:T(8,128)S(1)}, f32[64,128]{0,1:T(8,128)S(1)}, u32[]{:S(2)}, u32[]{:S(2)}) collective-permute-start(f32[64,128]{0,1:T(8,128)S(1)} %get-tuple-element.911), channel_id=1, source_target_pairs={{3,0},{4,1},{5,2},{6,3},{7,4},{0,5},{1,6},{2,7},{11,8},{12,9},{13,... | collective-permute-start | bytes 98312 | tf_op jit(solution)/shard_map/ppermute | solution.py:15
  161.3 72.6 %copy-start.4 = (f32[32,1024]{0,1:T(8,128)}, f32[32,1024]{0,1:T(8,128)S(1)}, u32[]{:S(2)}) copy-start(f32[32,1024]{0,1:T(8,128)S(1)} %get-tuple-element.899) | copy-start | bytes 393220
  162.6 22.9 %collective-permute-start.6 = (f32[32,128]{1,0:T(8,128)S(1)}, f32[32,128]{1,0:T(8,128)S(1)}, u32[]{:S(2)}, u32[]{:S(2)}) collective-permute-start(f32[32,128]{1,0:T(8,128)S(1)} %bitcast.327), channel_id=1, source_target_pairs={{7,0},{0,1},{1,2},{2,3},{3,4},{4,5},{5,6},{6,7},{15,8},{8,9},{9,10... | collective-permute-start | bytes 49160 | tf_op jit(solution)/shard_map/ppermute | solution.py:15
  162.6 26.1 %collective-permute-start.7 = (f32[32,128]{1,0:T(8,128)S(1)}, f32[32,128]{1,0:T(8,128)S(1)}, u32[]{:S(2)}, u32[]{:S(2)}) collective-permute-start(f32[32,128]{1,0:T(8,128)S(1)} %bitcast.321), channel_id=1, source_target_pairs={{1,0},{2,1},{3,2},{4,3},{5,4},{6,5},{7,6},{0,7},{9,8},{10,9},{11,1... | collective-permute-start | bytes 49160 | tf_op jit(solution)/shard_map/ppermute | solution.py:15
  168.0 21.3 %collective-permute-start.8 = (f32[32,128]{1,0:T(8,128)S(1)}, f32[32,128]{1,0:T(8,128)S(1)}, u32[]{:S(2)}, u32[]{:S(2)}) collective-permute-start(f32[32,128]{1,0:T(8,128)S(1)} %bitcast.317), channel_id=1, source_target_pairs={{6,0},{7,1},{0,2},{1,3},{2,4},{3,5},{4,6},{5,7},{14,8},{15,9},{8,1... | collective-permute-start | bytes 49160 | tf_op jit(solution)/shard_map/ppermute | solution.py:15
  168.0 21.9 %collective-permute-start.9 = (f32[32,128]{1,0:T(8,128)S(1)}, f32[32,128]{1,0:T(8,128)S(1)}, u32[]{:S(2)}, u32[]{:S(2)}) collective-permute-start(f32[32,128]{1,0:T(8,128)S(1)} %bitcast.313), channel_id=1, source_target_pairs={{2,0},{3,1},{4,2},{5,3},{6,4},{7,5},{0,6},{1,7},{10,8},{11,9},{12,... | collective-permute-start | bytes 49160 | tf_op jit(solution)/shard_map/ppermute | solution.py:15
  171.8 18.7 %collective-permute-start.10 = (f32[32,128]{1,0:T(8,128)S(1)}, f32[32,128]{1,0:T(8,128)S(1)}, u32[]{:S(2)}, u32[]{:S(2)}) collective-permute-start(f32[32,128]{1,0:T(8,128)S(1)} %bitcast.309), channel_id=1, source_target_pairs={{5,0},{6,1},{7,2},{0,3},{1,4},{2,5},{3,6},{4,7},{13,8},{14,9},{15,... | collective-permute-start | bytes 49160 | tf_op jit(solution)/shard_map/ppermute | solution.py:15
  185.5 5.7 %collective-permute-start.11 = (f32[32,128]{1,0:T(8,128)S(1)}, f32[32,128]{1,0:T(8,128)S(1)}, u32[]{:S(2)}, u32[]{:S(2)}) collective-permute-start(f32[32,128]{1,0:T(8,128)S(1)} %bitcast.307), channel_id=1, source_target_pairs={{3,0},{4,1},{5,2},{6,3},{7,4},{0,5},{1,6},{2,7},{11,8},{12,9},{13,... | collective-permute-start | bytes 49160 | tf_op jit(solution)/shard_map/ppermute | solution.py:15
  192.4 18.2 %copy-start.12 = (f32[8,384]{1,0:T(8,128)S(1)}, f32[8,384]{1,0:T(8,128)}, u32[]{:S(2)}) copy-start(f32[8,384]{1,0:T(8,128)} %mul.242) | copy-start | bytes 36868
  235.7 13.0 %collective-permute-start.12 = (f32[32,128]{1,0:T(8,128)S(1)}, f32[32,128]{1,0:T(8,128)S(1)}, u32[]{:S(2)}, u32[]{:S(2)}) collective-permute-start(f32[32,128]{1,0:T(8,128)S(1)} %bitcast.329), channel_id=1, source_target_pairs={{7,0},{0,1},{1,2},{2,3},{3,4},{4,5},{5,6},{6,7},{15,8},{8,9},{9,10... | collective-permute-start | bytes 49160 | tf_op jit(solution)/shard_map/ppermute | solution.py:15
  235.7 15.8 %collective-permute-start.13 = (f32[32,128]{1,0:T(8,128)S(1)}, f32[32,128]{1,0:T(8,128)S(1)}, u32[]{:S(2)}, u32[]{:S(2)}) collective-permute-start(f32[32,128]{1,0:T(8,128)S(1)} %bitcast.325), channel_id=1, source_target_pairs={{1,0},{2,1},{3,2},{4,3},{5,4},{6,5},{7,6},{0,7},{9,8},{10,9},{11,1... | collective-permute-start | bytes 49160 | tf_op jit(solution)/shard_map/ppermute | solution.py:15
  239.3 12.2 %collective-permute-start.14 = (f32[32,128]{1,0:T(8,128)S(1)}, f32[32,128]{1,0:T(8,128)S(1)}, u32[]{:S(2)}, u32[]{:S(2)}) collective-permute-start(f32[32,128]{1,0:T(8,128)S(1)} %bitcast.322), channel_id=1, source_target_pairs={{6,0},{7,1},{0,2},{1,3},{2,4},{3,5},{4,6},{5,7},{14,8},{15,9},{8,1... | collective-permute-start | bytes 49160 | tf_op jit(solution)/shard_map/ppermute | solution.py:15
  239.3 12.2 %collective-permute-start.15 = (f32[32,128]{1,0:T(8,128)S(1)}, f32[32,128]{1,0:T(8,128)S(1)}, u32[]{:S(2)}, u32[]{:S(2)}) collective-permute-start(f32[32,128]{1,0:T(8,128)S(1)} %bitcast.318), channel_id=1, source_target_pairs={{2,0},{3,1},{4,2},{5,3},{6,4},{7,5},{0,6},{1,7},{10,8},{11,9},{12,... | collective-permute-start | bytes 49160 | tf_op jit(solution)/shard_map/ppermute | solution.py:15
  243.1 8.4 %collective-permute-start.16 = (f32[32,128]{1,0:T(8,128)S(1)}, f32[32,128]{1,0:T(8,128)S(1)}, u32[]{:S(2)}, u32[]{:S(2)}) collective-permute-start(f32[32,128]{1,0:T(8,128)S(1)} %bitcast.314), channel_id=1, source_target_pairs={{5,0},{6,1},{7,2},{0,3},{1,4},{2,5},{3,6},{4,7},{13,8},{14,9},{15,... | collective-permute-start | bytes 49160 | tf_op jit(solution)/shard_map/ppermute | solution.py:15
  248.7 4.3 collective-permute-start.17
  287.9 126.6 %copy-start = (f32[32,1024]{0,1:T(8,128)}, f32[32,1024]{0,1:T(8,128)S(1)}, u32[]{:S(2)}) copy-start(f32[32,1024]{0,1:T(8,128)S(1)} %get-tuple-element.897) | copy-start | bytes 393220
  307.6 14.0 %collective-permute-start.18 = (f32[64,128]{0,1:T(8,128)S(1)}, f32[64,128]{0,1:T(8,128)S(1)}, u32[]{:S(2)}, u32[]{:S(2)}) collective-permute-start(f32[64,128]{0,1:T(8,128)S(1)} %get-tuple-element.910), channel_id=1, source_target_pairs={{7,0},{0,1},{1,2},{2,3},{3,4},{4,5},{5,6},{6,7},{15,8},{8,9},{9,10... | collective-permute-start | bytes 98312 | tf_op jit(solution)/shard_map/ppermute | solution.py:15
  308.6 16.2 %collective-permute-start.19 = (f32[64,128]{0,1:T(8,128)S(1)}, f32[64,128]{0,1:T(8,128)S(1)}, u32[]{:S(2)}, u32[]{:S(2)}) collective-permute-start(f32[64,128]{0,1:T(8,128)S(1)} %get-tuple-element.909), channel_id=1, source_target_pairs={{1,0},{2,1},{3,2},{4,3},{5,4},{6,5},{7,6},{0,7},{9,8},{10,9},{11,1... | collective-permute-start | bytes 98312 | tf_op jit(solution)/shard_map/ppermute | solution.py:15
  312.2 13.3 %collective-permute-start.20 = (f32[64,128]{0,1:T(8,128)S(1)}, f32[64,128]{0,1:T(8,128)S(1)}, u32[]{:S(2)}, u32[]{:S(2)}) collective-permute-start(f32[64,128]{0,1:T(8,128)S(1)} %get-tuple-element.908), channel_id=1, source_target_pairs={{6,0},{7,1},{0,2},{1,3},{2,4},{3,5},{4,6},{5,7},{14,8},{15,9},{8,1... | collective-permute-start | bytes 98312 | tf_op jit(solution)/shard_map/ppermute | solution.py:15
  312.2 13.9 %collective-permute-start.21 = (f32[64,128]{0,1:T(8,128)S(1)}, f32[64,128]{0,1:T(8,128)S(1)}, u32[]{:S(2)}, u32[]{:S(2)}) collective-permute-start(f32[64,128]{0,1:T(8,128)S(1)} %get-tuple-element.907), channel_id=1, source_target_pairs={{2,0},{3,1},{4,2},{5,3},{6,4},{7,5},{0,6},{1,7},{10,8},{11,9},{12,... | collective-permute-start | bytes 98312 | tf_op jit(solution)/shard_map/ppermute | solution.py:15
  316.0 10.7 %collective-permute-start.22 = (f32[64,128]{0,1:T(8,128)S(1)}, f32[64,128]{0,1:T(8,128)S(1)}, u32[]{:S(2)}, u32[]{:S(2)}) collective-permute-start(f32[64,128]{0,1:T(8,128)S(1)} %get-tuple-element.906), channel_id=1, source_target_pairs={{5,0},{6,1},{7,2},{0,3},{1,4},{2,5},{3,6},{4,7},{13,8},{14,9},{15,... | collective-permute-start | bytes 98312 | tf_op jit(solution)/shard_map/ppermute | solution.py:15
  317.7 10.3 %copy-start.42 = (f32[64,1]{0,1:T(1,128)S(1)}, f32[64,1]{0,1:T(1,128)}, u32[]{:S(2)}) copy-start(f32[64,1]{0,1:T(1,128)} %copy-done.41) | copy-start | bytes 772
  321.5 5.8 %collective-permute-start.23 = (f32[64,128]{0,1:T(8,128)S(1)}, f32[64,128]{0,1:T(8,128)S(1)}, u32[]{:S(2)}, u32[]{:S(2)}) collective-permute-start(f32[64,128]{0,1:T(8,128)S(1)} %get-tuple-element.905), channel_id=1, source_target_pairs={{3,0},{4,1},{5,2},{6,3},{7,4},{0,5},{1,6},{2,7},{11,8},{12,9},{13,... | collective-permute-start | bytes 98312 | tf_op jit(solution)/shard_map/ppermute | solution.py:15
  334.6 17.1 %copy-start.11 = (f32[32,3072]{1,0:T(8,128)S(1)}, f32[32,3072]{1,0:T(8,128)}, u32[]{:S(2)}) copy-start(f32[32,3072]{1,0:T(8,128)} %param.48) | copy-start | bytes 1179652
  334.6 17.1 %copy-start.24 = (f32[3072]{0:T(1024)S(1)}, f32[3072]{0:T(1024)}, u32[]{:S(2)}) copy-start(f32[3072]{0:T(1024)} %param.49) | copy-start | bytes 36868
  376.0 10.7 %copy-start.13 = (f32[8,384]{1,0:T(8,128)S(1)}, f32[8,384]{1,0:T(8,128)}, u32[]{:S(2)}) copy-start(f32[8,384]{1,0:T(8,128)} %mul.242) | copy-start | bytes 36868
  419.4 12.2 %collective-permute-start.24 = (f32[32,128]{1,0:T(8,128)S(1)}, f32[32,128]{1,0:T(8,128)}, u32[]{:S(2)}, u32[]{:S(2)}) collective-permute-start(f32[32,128]{1,0:T(8,128)S(1)} %bitcast.328), channel_id=1, source_target_pairs={{7,0},{0,1},{1,2},{2,3},{3,4},{4,5},{5,6},{6,7},{15,8},{8,9},{9,10... | collective-permute-start | bytes 49160 | tf_op jit(solution)/shard_map/ppermute | solution.py:15
  420.2 14.8 %collective-permute-start.25 = (f32[32,128]{1,0:T(8,128)S(1)}, f32[32,128]{1,0:T(8,128)}, u32[]{:S(2)}, u32[]{:S(2)}) collective-permute-start(f32[32,128]{1,0:T(8,128)S(1)} %bitcast.324), channel_id=1, source_target_pairs={{1,0},{2,1},{3,2},{4,3},{5,4},{6,5},{7,6},{0,7},{9,8},{10,9},{11,1... | collective-permute-start | bytes 49160 | tf_op jit(solution)/shard_map/ppermute | solution.py:15
  423.7 12.0 %collective-permute-start.26 = (f32[32,128]{1,0:T(8,128)S(1)}, f32[32,128]{1,0:T(8,128)}, u32[]{:S(2)}, u32[]{:S(2)}) collective-permute-start(f32[32,128]{1,0:T(8,128)S(1)} %bitcast.320), channel_id=1, source_target_pairs={{6,0},{7,1},{0,2},{1,3},{2,4},{3,5},{4,6},{5,7},{14,8},{15,9},{8,1... | collective-permute-start | bytes 49160 | tf_op jit(solution)/shard_map/ppermute | solution.py:15
  423.7 12.7 %collective-permute-start.27 = (f32[32,128]{1,0:T(8,128)S(1)}, f32[32,128]{1,0:T(8,128)S(1)}, u32[]{:S(2)}, u32[]{:S(2)}) collective-permute-start(f32[32,128]{1,0:T(8,128)S(1)} %bitcast.316), channel_id=1, source_target_pairs={{2,0},{3,1},{4,2},{5,3},{6,4},{7,5},{0,6},{1,7},{10,8},{11,9},{12,... | collective-permute-start | bytes 49160 | tf_op jit(solution)/shard_map/ppermute | solution.py:15
  427.5 8.9 %collective-permute-start.28 = (f32[32,128]{1,0:T(8,128)S(1)}, f32[32,128]{1,0:T(8,128)S(1)}, u32[]{:S(2)}, u32[]{:S(2)}) collective-permute-start(f32[32,128]{1,0:T(8,128)S(1)} %bitcast.312), channel_id=1, source_target_pairs={{5,0},{6,1},{7,2},{0,3},{1,4},{2,5},{3,6},{4,7},{13,8},{14,9},{15,... | collective-permute-start | bytes 49160 | tf_op jit(solution)/shard_map/ppermute | solution.py:15
  431.6 4.8 collective-permute-start.29
  468.7 13.0 %collective-permute-start.30 = (f32[32,128]{1,0:T(8,128)S(1)}, f32[32,128]{1,0:T(8,128)S(1)}, u32[]{:S(2)}, u32[]{:S(2)}) collective-permute-start(f32[32,128]{1,0:T(8,128)S(1)} %bitcast.330), channel_id=1, source_target_pairs={{7,0},{0,1},{1,2},{2,3},{3,4},{4,5},{5,6},{6,7},{15,8},{8,9},{9,10... | collective-permute-start | bytes 49160 | tf_op jit(solution)/shard_map/ppermute | solution.py:15
  468.7 15.8 %collective-permute-start.31 = (f32[32,128]{1,0:T(8,128)S(1)}, f32[32,128]{1,0:T(8,128)S(1)}, u32[]{:S(2)}, u32[]{:S(2)}) collective-permute-start(f32[32,128]{1,0:T(8,128)S(1)} %bitcast.326), channel_id=1, source_target_pairs={{1,0},{2,1},{3,2},{4,3},{5,4},{6,5},{7,6},{0,7},{9,8},{10,9},{11,1... | collective-permute-start | bytes 49160 | tf_op jit(solution)/shard_map/ppermute | solution.py:15
  472.3 12.2 %collective-permute-start.32 = (f32[32,128]{1,0:T(8,128)S(1)}, f32[32,128]{1,0:T(8,128)S(1)}, u32[]{:S(2)}, u32[]{:S(2)}) collective-permute-start(f32[32,128]{1,0:T(8,128)S(1)} %bitcast.323), channel_id=1, source_target_pairs={{6,0},{7,1},{0,2},{1,3},{2,4},{3,5},{4,6},{5,7},{14,8},{15,9},{8,1... | collective-permute-start | bytes 49160 | tf_op jit(solution)/shard_map/ppermute | solution.py:15
  472.3 12.2 %collective-permute-start.33 = (f32[32,128]{1,0:T(8,128)S(1)}, f32[32,128]{1,0:T(8,128)S(1)}, u32[]{:S(2)}, u32[]{:S(2)}) collective-permute-start(f32[32,128]{1,0:T(8,128)S(1)} %bitcast.319), channel_id=1, source_target_pairs={{2,0},{3,1},{4,2},{5,3},{6,4},{7,5},{0,6},{1,7},{10,8},{11,9},{12,... | collective-permute-start | bytes 49160 | tf_op jit(solution)/shard_map/ppermute | solution.py:15
  476.1 8.4 %collective-permute-start.34 = (f32[32,128]{1,0:T(8,128)S(1)}, f32[32,128]{1,0:T(8,128)S(1)}, u32[]{:S(2)}, u32[]{:S(2)}) collective-permute-start(f32[32,128]{1,0:T(8,128)S(1)} %bitcast.315), channel_id=1, source_target_pairs={{5,0},{6,1},{7,2},{0,3},{1,4},{2,5},{3,6},{4,7},{13,8},{14,9},{15,... | collective-permute-start | bytes 49160 | tf_op jit(solution)/shard_map/ppermute | solution.py:15
  481.7 4.3 collective-permute-start.35
  (31 other events, 151.6 us)
